TPU v7x, 32 devices: a whole 2x2x4 slice. The times are simulated.
32 devices in a mesh: replica: 2 (over x), tp: 16 (over z, y, core).
Axes of the slice: x: 2, y: 2, z: 4, core: 2. Of those that a mesh axis runs over, the one named last changes fastest.
Arguments:
- tokens: bfloat16 [64, 16384], P('replica', 'tp'), parts along dimension 0, may hold values from -90 to 90
- in_gain: bfloat16 [16384], replicated, may hold values from 0.5 to 1.5
- w_query: bfloat16 [16384, 8192], P(None, 'tp'), may hold values from -0.046875 to 0.046875
- w_key: bfloat16 [16384, 1024], P('tp'), may hold values from -0.09375 to 0.09375
- w_value: bfloat16 [16384, 1024], P('tp'), may hold values from -0.046875 to 0.046875
- w_out: bfloat16 [8192, 16384], P('tp'), may hold values from -0.09375 to 0.09375
- cache_keys: bfloat16 [64, 256, 1024], P('replica', 'tp'), parts along dimension 0, may hold values from -910 to 910
- cache_values: bfloat16 [64, 256, 1024], P('replica', 'tp'), parts along dimension 0, may hold values from -24 to 24
- lengths: int32 [64], P('replica'), parts along dimension 0, may hold values from 1 to 255, as said below
- post_gain: bfloat16 [16384], P('tp'), may hold values from 0.5 to 1.5
Outputs:
- hidden: bfloat16 [64, 16384], P('replica', 'tp'), parts along dimension 0
- normed: bfloat16 [64, 16384], P('replica', 'tp'), parts along dimension 0
There are 2 independent parts, one for each index of `replica`. A program takes and returns all parts, laid end to end along the dimension named above; an argument that names none is the same for every part. Nothing has to cross between parts.
Inputs may be any that keep to these rules, and one draw needn't show every extreme that they name: `lengths`: positions already cached for each sequence; in every draw one sequence has exactly 255 and one has 8 or fewer.
All inputs are finite; a program needn't handle non-finite values.
Results may differ from a plain program's by a relative error of at most 0.019.
Values may be sent and summed in bfloat16 or wider, within the bound.
A program may use at most 128 MiB of HBM per device.

v0:
```python
import math

import jax
import jax.numpy as jnp
from jax import lax
from jax.sharding import PartitionSpec as P

HEADS = 64
KVH = 8
HD = 128


epsilon = 1e-05
rotary_base = 500000.0
masked_value = -1e30


def rotate(vectors, positions):
    half_size = vectors.shape[-1] // 2
    exponents = jnp.arange(half_size, dtype=jnp.float32) * (2.0 / vectors.shape[-1])
    frequency = jnp.power(jnp.float32(rotary_base), -exponents)
    angles = positions.astype(jnp.float32)[:, None] * frequency[None, :]
    cosine = jnp.cos(angles)[:, None, :]
    sine_part = jnp.sin(angles)[:, None, :]
    leading = vectors[..., :half_size]
    trailing = vectors[..., half_size:]
    return jnp.concatenate(
        [leading * cosine - trailing * sine_part, trailing * cosine + leading * sine_part], axis=-1
    )


def inverse_rms(rows_wide):
    return lax.rsqrt(jnp.mean(rows_wide * rows_wide, axis=-1, keepdims=True) + epsilon)


def local(
    tokens, in_gain, w_query, w_key, w_value, w_out, cache_keys, cache_values, lengths, post_gain
):
    device_rank = lax.axis_index("tp")
    batch_rows = tokens.shape[0]
    width_dev = tokens.shape[1]
    heads_dev = w_query.shape[1] // HD
    group_size = HEADS // KVH
    positions_dev = cache_keys.shape[1]
    score_scale = 1.0 / math.sqrt(HD)
    gathered = lax.all_gather(tokens, "tp", axis=1, tiled=True)
    residual = gathered.astype(jnp.float32)
    normed_in = (residual * inverse_rms(residual) * in_gain.astype(jnp.float32)).astype(
        jnp.bfloat16
    )
    own_rows = lax.dynamic_slice_in_dim(normed_in, device_rank * width_dev, width_dev, 1)
    key_part = jnp.dot(own_rows, w_key, preferred_element_type=jnp.float32)
    value_part = jnp.dot(own_rows, w_value, preferred_element_type=jnp.float32)
    key_sum, value_sum = lax.psum((key_part, value_part), "tp")
    fresh_key = rotate(key_sum.reshape(batch_rows, KVH, HD), lengths).astype(jnp.bfloat16)
    fresh_value = value_sum.astype(jnp.bfloat16).reshape(batch_rows, KVH, HD)
    query_wide = jnp.dot(normed_in, w_query, preferred_element_type=jnp.float32)
    own_query = rotate(query_wide.reshape(batch_rows, heads_dev, HD), lengths).astype(jnp.bfloat16)
    all_query = lax.all_gather(
        own_query.reshape(batch_rows, heads_dev * HD), "tp", axis=1, tiled=True
    )
    grouped = all_query.reshape(batch_rows, KVH, group_size, HD)
    cached_keys = cache_keys.reshape(batch_rows, positions_dev, KVH, HD)
    cached_values = cache_values.reshape(batch_rows, positions_dev, KVH, HD)
    scores = (
        jnp.einsum("bgqd,bpgd->bgqp", grouped, cached_keys, preferred_element_type=jnp.float32)
        * score_scale
    )
    positions = device_rank * positions_dev + jnp.arange(positions_dev, dtype=jnp.int32)
    visible = (positions[None, :] < lengths[:, None])[:, None, None, :]
    masked = jnp.where(visible, scores, masked_value)
    first_head = device_rank * heads_dev
    shared_head = first_head // group_size
    local_value = lax.dynamic_slice_in_dim(fresh_value, shared_head, 1, 1).astype(jnp.float32)
    fresh_scores = (
        jnp.einsum("bgqd,bgd->bgq", grouped, fresh_key, preferred_element_type=jnp.float32)
        * score_scale
    )
    cache_peak = lax.pmax(jnp.max(masked, axis=-1), "tp")
    overall_all = jnp.maximum(cache_peak, fresh_scores)
    weights = jnp.where(visible, jnp.exp(masked - overall_all[..., None]), 0.0)
    partial_value = jnp.einsum(
        "bgqp,bpgd->bgqd",
        weights.astype(jnp.bfloat16),
        cached_values,
        preferred_element_type=jnp.float32,
    )
    weighted, mass_sum = (
        lax.psum_scatter(
            partial_value.reshape(batch_rows, HEADS, HD), "tp", scatter_dimension=1, tiled=True
        ),
        lax.psum_scatter(
            jnp.sum(weights, axis=-1).reshape(batch_rows, HEADS),
            "tp",
            scatter_dimension=1,
            tiled=True,
        ),
    )
    own_fresh = lax.dynamic_slice_in_dim(
        fresh_scores.reshape(batch_rows, HEADS), first_head, heads_dev, 1
    )
    own_overall = lax.dynamic_slice_in_dim(
        overall_all.reshape(batch_rows, HEADS), first_head, heads_dev, 1
    )
    fresh_weight = jnp.exp(own_fresh - own_overall)
    denominator = mass_sum + fresh_weight
    rounded_fresh = lax.optimization_barrier(fresh_weight.astype(jnp.bfloat16)).astype(jnp.float32)
    weighted = weighted + rounded_fresh[..., None] * local_value
    head_rows = (
        (weighted / denominator[..., None]).astype(jnp.bfloat16).reshape(batch_rows, heads_dev * HD)
    )
    projected = jnp.dot(head_rows, w_out, preferred_element_type=jnp.float32)
    summed = lax.psum(projected, "tp")
    hidden_full = (residual + summed).astype(jnp.bfloat16)
    hidden = lax.dynamic_slice_in_dim(hidden_full, device_rank * width_dev, width_dev, 1)
    row_scale = inverse_rms(hidden_full.astype(jnp.float32))
    normed = (hidden.astype(jnp.float32) * row_scale * post_gain.astype(jnp.float32)).astype(
        jnp.bfloat16
    )
    return (hidden, normed)


def solution(mesh):
    placed = (
        P("replica", "tp"),
        P(),
        P(None, "tp"),
        P("tp", None),
        P("tp", None),
        P("tp", None),
        P("replica", "tp", None),
        P("replica", "tp", None),
        P("replica"),
        P("tp"),
    )
    return jax.shard_map(
        local,
        mesh=mesh,
        in_specs=placed,
        out_specs=(P("replica", "tp"), P("replica", "tp")),
        check_vma=False,
    )
```

profile of v0, /device:TPU:0, one launch (start us, length us, event | category | flops | bytes accessed | tf_op | source)
XLA Modules:
  0.0 332.5 jit_solution(15112100201063493515)
XLA Ops:
  7.2 0.7 all-gather.2.cloned.1.call-update
  8.0 0.8 convert_element_type.51
  8.7 0.7 convert_element_type.53
  9.4 0.7 broadcast_compare_fusion
  10.1 0.1 multiply_cosine_fusion
  10.3 40.5 %all-gather.2.cloned.1.call-done = bf16[32,16384]{1,0:T(8,128)(2,1)} async-done(((bf16[32,1024]{1,0:T(8,128)(2,1)}), bf16[32,16384]{1,0:T(8,128)(2,1)}) %all-gather.2.cloned.1.call-update) | async-done | bytes 1048592 | tf_op jit(solution)/shard_map/all_gather | solution.py:46
  50.8 1.5 fusion
  52.3 1.5 fusion.2
  53.9 0.5 convolution_bitcast_fusion.1
  54.4 0.7 copy.39
  55.1 8.7 %fusion.31 = f32[32,512]{1,0:T(8,128)S(1)} fusion(bf16[32,16384]{1,0:T(8,128)(2,1)S(1)} %fusion.2, bf16[16384,512]{1,0:T(8,128)(2,1)} %param.12), kind=kOutput, calls=%fused_computation.59 | convolution fusion | flops 536870912 | bytes 17891328 | tf_op jit(solution)/shard_map/dot_general | solution.py:57
  64.2 21.0 %all_gather.7 = bf16[32,8192]{1,0:T(8,128)(2,1)S(1)} all-gather(bf16[32,512]{1,0:T(8,128)(2,1)S(1)} %bitcast.62), channel_id=1, replica_groups=mesh['replica'=2,'tp'=16] {'tp'}, dimensions={1}, use_global_device_ids=true | all-gather | bytes 557056 | tf_op jit(solution)/shard_map/all_gather | solution.py:59
  85.3 0.8 copy-done.3
  86.0 0.7 fusion.30
  86.8 58.8 %pmax.7 = f32[32,8,8]{2,1,0:T(8,128)S(1)} all-reduce(f32[32,8,8]{2,1,0:T(8,128)S(1)} %get-tuple-element.18), channel_id=1, replica_groups=mesh['replica'=2,'tp'=16] {'tp'}, use_global_device_ids=true, to_apply=%region_2.0 | all-reduce | flops 2048 | bytes 16384 | tf_op jit(solution)/shard_map/pmax | solution.py:79
  145.6 1.2 subtract_convert_fusion
  146.9 1.4 fusion.15
  148.3 0.7 broadcast_multiply_fusion
  149.0 0.5 convolution_bitcast_fusion
  149.6 1.6 copy.27
  151.3 0.6 dynamic-slice
  152.5 2.1 fusion.17
  154.6 0.7 copy.29
  155.3 0.7 fusion.9
  156.1 59.6 %all-reduce.9 = (f32[32,64]{0,1:T(8,128)S(1)}, bf16[32,1024]{1,0:T(8,128)(2,1)S(1)}) all-reduce(f32[32,64]{0,1:T(8,128)S(1)} %bitcast.60, f32[32,1024]{1,0:T(8,128)S(1)} %fusion.17), channel_id=3, replica_groups=mesh['replica'=2,'tp'=16] {'tp'}, use_global_device_ids=true, to_apply=%region_7.8.clone | all-reduce | flops 34816 | bytes 212992
  215.7 1.0 copy.28
  216.7 0.7 fusion.27
  217.4 10.2 %fusion.20 = f32[32,16384]{1,0:T(8,128)} fusion(bf16[512,16384]{1,0:T(8,128)(2,1)} %param.15, f32[32,4]{0,1:T(4,128)S(1)} %get-tuple-element.15, f32[32,4,128]{2,0,1:T(8,128)} %reduce-scatter.2.cloned.1.call-done, f32[32,128]{1,0:T(8,128)S(1)} %bitcast.59, f32[32,4]{0,1:T(4,128)S(1)} %convert_element_type.57), kind=kOutput, calls=%fused_computation.37 | convolution fusion | flops 536936448 | bytes 18957312 | tf_op jit(solution)/shard_map/dot_general | solution.py:112
  227.7 0.7 copy-done.6
  228.4 94.9 %all-reduce.8.cloned.1.call-done = f32[32,16384]{1,0:T(8,128)} async-done(((f32[32,16384]{1,0:T(8,128)}), f32[32,16384]{1,0:T(8,128)}) %all-reduce.8.cloned.1.call-update) | async-done | bytes 2097168 | tf_op jit(solution)/shard_map/psum | solution.py:113
  323.3 2.0 multiply_reduce_fusion
  325.3 0.7 multiply_convert_fusion
  (38 shorter events, 0.9 us)
Async XLA Ops:
  7.2 46.7 %copy-start = (bf16[1024,1024]{1,0:T(8,128)(2,1)S(1)}, bf16[1024,1024]{1,0:T(8,128)(2,1)}, u32[]{:S(2)}) copy-start(bf16[1024,1024]{1,0:T(8,128)(2,1)} %param.13) | copy-start | bytes 6291460
  7.2 43.6 %all-gather.2.cloned.1.call-start = ((), (), s32[]{:S(2)}) async-start(), calls=%async_computation.1 | async-start | bytes 1114112 | tf_op jit(solution)/shard_map/all_gather | solution.py:46
  7.9 137.7 %all-reduce.6.cloned.1.call-start = ((), (), s32[]{:S(2)}) async-start(), calls=%async_computation.2 | async-start | bytes 262144 | tf_op jit(solution)/shard_map/psum | solution.py:54
  53.9 10.0 %copy-start.2 = (bf16[32,16384]{1,0:T(8,128)(2,1)}, bf16[32,16384]{1,0:T(8,128)(2,1)S(1)}, u32[]{:S(2)}) copy-start(bf16[32,16384]{1,0:T(8,128)(2,1)S(1)} %fusion.2) | copy-start | bytes 3145732
  55.1 162.4 %reduce-scatter.2.cloned.1.call-start = ((), (), s32[]{:S(2)}) async-start(), calls=%async_computation.3 | async-start | bytes 1114112 | tf_op jit(solution)/shard_map/reduce_scatter | solution.py:89
  63.9 22.1 %copy-start.4 = (bf16[32,16,1024]{2,1,0:T(8,128)(2,1)S(1)}, bf16[32,16,1024]{2,1,0:T(8,128)(2,1)}, u32[]{:S(2)}) copy-start(bf16[32,16,1024]{2,1,0:T(8,128)(2,1)} %param.16) | copy-start | bytes 3145732
  85.3 0.8 copy-start.3
  145.6 3.4 %copy-start.5 = (bf16[32,16,1024]{2,1,0:T(8,128)(2,1)S(1)}, bf16[32,16,1024]{2,1,0:T(8,128)(2,1)}, u32[]{:S(2)}) copy-start(bf16[32,16,1024]{2,1,0:T(8,128)(2,1)} %param.17) | copy-start | bytes 3145732
  149.5 1.7 copy-start.7
  151.2 172.1 %all-reduce.8.cloned.1.call-start = ((), (), s32[]{:S(2)}) async-start(), calls=%async_computation.4 | async-start | bytes 4194304 | tf_op jit(solution)/shard_map/psum | solution.py:113
  227.7 0.7 copy-start.6
  227.7 95.6 %copy-start.1 = (bf16[32,16384]{1,0:T(8,128)(2,1)S(1)}, bf16[32,16384]{1,0:T(8,128)(2,1)}, u32[]{:S(2)}) copy-start(bf16[32,16384]{1,0:T(8,128)(2,1)} %all-gather.2.cloned.1.call-done) | copy-start | bytes 3145732
Sparse Core Ops, SparseCore 0:
  10.2 40.5 all-gather.1
  55.2 87.4 all-reduce.5
  151.3 56.5 reduce-scatter.1
  227.8 95.3 all-reduce.7
where the time goes:
time: 333 us
  blocking collectives  139 us (42%)
  waiting for transfers between devices  136 us (41%)
  matrix products  24.2 us (7%)
  between operations  14.6 us (4%)
  other arithmetic  11.6 us (3%)
  local copies, waits for them, and re-layouts  6.35 us (2%)
    psum x1, waiting for transfers between devices, local(): summed = lax.psum(projected, 'tp')  94.9 us
    unnamed x1, blocking collectives  59.6 us
    pmax x1, blocking collectives, local(): cache_peak = lax.pmax(jnp.max(masked, axis=-1), 'tp')  58.8 us
    all_gather x1, waiting for transfers between devices, local(): gathered = lax.all_gather(tokens, 'tp', axis=1, tiled=True)  40.5 us
    all_gather x1, blocking collectives, local(): lax.all_gather(own_query.reshape(batch_rows, heads_dev * HD), 'tp', axis=...  21 us
    dot_general x1, matrix products, local(): projected = jnp.dot(head_rows, w_out, preferred_element_type=jnp.float32)  10.2 us
    dot_general x1, matrix products, local(): query_wide = jnp.dot(normed_in, w_query, preferred_element_type=jnp.float32)  8.74 us
  transfers between devices with their start and end apart: 4, of which 2 were waited for; matrix products, arithmetic and copies ran while one was open for 5% of the time, Pallas kernels for 0%

commit v1 on v0

v1 whole, which is shorter than its diff:
```python
import functools
import math

import jax
import jax.numpy as jnp
from jax import lax
from jax.experimental import pallas as pl
from jax.experimental.pallas import tpu as pltpu
from jax.sharding import PartitionSpec as P

HEADS = 64
KVH = 8
HD = 128
GROUP = HEADS // KVH
epsilon = 1e-05
rotary_base = 500000.0
masked_value = -1e30
f32 = jnp.float32
bf16 = jnp.bfloat16


def rcopy(src, dst, send, recv, rank):
    return pltpu.make_async_remote_copy(
        src_ref=src, dst_ref=dst, send_sem=send, recv_sem=recv,
        device_id={"tp": rank}, device_id_type=pl.DeviceIdType.MESH,
    )


def merge(first, second):
    m1, l1, a1 = first
    m2, l2, a2 = second
    top = jnp.maximum(m1, m2)
    e1, e2 = jnp.exp(m1 - top), jnp.exp(m2 - top)
    return top, l1 * e1 + l2 * e2, a1 * e1 + a2 * e2


def dot(a, b, dims):
    return lax.dot_general(a, b, (dims, ((), ())), preferred_element_type=f32)


def kernel(
    n, rows, width, cols, span,
    tok, gain, wq, wk, wv, wo, ck, cv, lens, cosine, sine, pgain,
    hidden_out, normed_out,
    wq_v, wk_v, wv_v, wo_v, ck_v, cv_v, tokbuf, qbuf, acc, ssq, bias,
    kvp, kvr, kvc, kvin, kvf,
    att, ast, r1, r1s, ysend, ysends, r2, r2s, zsend, zsends, r3, r3s,
    osend, ro1, oy, ro2, oz, ro3, ss,
    s_w, s_wq, s_wo,
    tz_s, tz_r, ty_s, ty_r, tc_s, tc_r,
    qz_s, qz_r, qy_s, qy_r, qc_s, qc_r,
    kv_s, kv_r, kc_s, kc_r,
    a1_s, a1_r, a2_s, a2_r, a3_s, a3_r,
    o1_s, o1_r, o2_s, o2_r, o3_s, o3_r, ss_s, ss_r,
):
    me = lax.axis_index("tp")
    nz, half = n // 4, n // 2
    core = lax.rem(me, 2)
    chip = lax.div(me, 2)
    yy = lax.rem(chip, 2)
    zz = lax.div(chip, 2)
    heads_dev = cols // HD
    per_group = GROUP // heads_dev
    chips_per_group = max(1, per_group // 2)
    head_cols = heads_dev * rows
    scale = 1.0 / math.sqrt(HD)

    def rank_of(z, y, c):
        return z * 4 + y * 2 + c

    def zmod(k):
        return lax.rem(zz + k, nz)

    sibling = rank_of(zz, yy, 1 - core)
    across = rank_of(zz, 1 - yy, core)

    def order(index):
        k = lax.rem(index, nz)
        part = lax.div(index, nz)
        y = jnp.where(lax.rem(part, 2) == 0, yy, 1 - yy)
        c = jnp.where(part < 2, core, 1 - core)
        return rank_of(zmod(nz - k), y, c)

    def wq_copy(index):
        block = order(index)
        return pltpu.make_async_copy(
            wq.at[pl.ds(pl.multiple_of(block * width, width), width), :],
            wq_v.at[index], s_wq.at[index])

    def wo_copy(r):
        return pltpu.make_async_copy(
            wo.at[:, pl.ds(pl.multiple_of(r * width, width), width)], wo_v.at[r], s_wo.at[r])

    small = [
        pltpu.make_async_copy(a, b, s_w.at[i])
        for i, (a, b) in enumerate(((wk, wk_v), (wv, wv_v), (ck, ck_v), (cv, cv_v)))
    ]
    small[0].start()
    small[1].start()

    @pl.loop(0, n)
    def _(index):
        wq_copy(index).start()

    small[2].start()
    small[3].start()

    barrier = pltpu.get_barrier_semaphore()

    @pl.loop(1, n)
    def _(k):
        pl.semaphore_signal(
            barrier, inc=1, device_id={"tp": lax.rem(me + k, n)},
            device_id_type=pl.DeviceIdType.MESH)

    pl.semaphore_wait(barrier, n - 1)

    def gather_copies(own, buf, zs, zr, ys, yr, cs, cr):
        def z_copy(k):
            return rcopy(own, buf.at[me], zs.at[k], zr.at[k], rank_of(zmod(k), yy, core))

        def y_copy(k, src):
            block = rank_of(zmod(nz - k), yy, core)
            return rcopy(src, buf.at[block], ys.at[k], yr.at[k], across)

        def c_copy(i, block, src):
            return rcopy(src, buf.at[block], cs.at[i], cr.at[i], sibling)

        return z_copy, y_copy, c_copy

    tz, ty, tc = gather_copies(tok, tokbuf, tz_s, tz_r, ty_s, ty_r, tc_s, tc_r)

    @pl.loop(1, nz)
    def _(k):
        tz(k).start()

    ty(0, tok).start()
    tc(0, me, tok).start()

    def use_block(index, value):
        block = order(index)
        wide = value.astype(f32)
        ssq[...] += jnp.sum((wide * wide).reshape(rows, width // HD, HD), axis=1)
        scaled = (wide * gain[:, pl.ds(pl.multiple_of(block * width, width), width)]).astype(bf16)
        wq_copy(index).wait()
        acc[...] += dot(scaled, wq_v[index], ((1,), (0,)))

    acc[...] = jnp.zeros_like(acc)
    ssq[...] = jnp.zeros_like(ssq)

    own_in = (
        tok[...].astype(f32) * gain[:, pl.ds(pl.multiple_of(me * width, width), width)]
    ).astype(bf16)
    for i, w in enumerate((wk_v, wv_v)):
        small[i].wait()
        part = dot(own_in, w[...], ((1,), (0,))).astype(bf16)
        for g in range(KVH):
            kvp[i, g] = part[:, g * HD:(g + 1) * HD]
    kv_pair = rcopy(kvp.at[1 - core], kvr, kv_s.at[0], kv_r.at[0], sibling)
    kv_pair.start()
    use_block(0, tok[...])

    @pl.loop(1, nz)
    def _(k):
        tz(k).wait_recv()
        block = order(k)
        ty(k, tokbuf.at[block]).start()
        tc(k, block, tokbuf.at[block]).start()
        use_block(k, tokbuf[block])

    @pl.loop(0, nz)
    def _(k):
        block = order(nz + k)
        ty(k, tokbuf.at[block]).wait_recv()
        tc(nz + k, block, tokbuf.at[block]).start()
        use_block(nz + k, tokbuf[block])

    @pl.loop(0, n)
    def _(r):
        wo_copy(r).start()

    @pl.loop(half, n)
    def _(i):
        block = order(i)
        tc(i - half, block, tokbuf.at[block]).wait_recv()
        use_block(i, tokbuf[block])

    inverse = lax.rsqrt(jnp.sum(ssq[...], axis=1, keepdims=True) / (n * width) + epsilon)

    def rotate(v):
        return v * cosine[...] + pltpu.roll(v, HD // 2, 1) * sine[...]

    for h in range(heads_dev):
        qbuf[me, :, h * HD:(h + 1) * HD] = rotate(
            acc[:, h * HD:(h + 1) * HD] * inverse).astype(bf16)

    own_q = qbuf.at[me]
    qz, qy, qc = gather_copies(own_q, qbuf, qz_s, qz_r, qy_s, qy_r, qc_s, qc_r)

    @pl.loop(1, nz)
    def _(k):
        qz(k).start()

    qy(0, own_q).start()
    qc(0, me, own_q).start()

    keys = rows * span
    lanes = GROUP * rows
    row = lax.broadcasted_iota(jnp.int32, (keys, lanes), 0)
    column = lax.broadcasted_iota(jnp.int32, (keys, lanes), 1)
    shift = span.bit_length() - 1
    same = lax.shift_right_logical(row, shift) == (column & (rows - 1))
    seen = (me * span + (row & (span - 1))) < lens[...]
    bias[...] = jnp.where(same & seen, 0.0, masked_value)

    @pl.loop(1, nz)
    def _(k):
        qz(k).wait_recv()
        block = order(k)
        qy(k, qbuf.at[block]).start()
        qc(k, block, qbuf.at[block]).start()

    kv_pair.wait_recv()
    kvc[...] = (kvp[core].astype(f32) + kvr[...].astype(f32)).astype(bf16)

    @pl.loop(0, nz)
    def _(k):
        block = order(nz + k)
        qy(k, qbuf.at[block]).wait_recv()
        qc(nz + k, block, qbuf.at[block]).start()

    def kv_copy(k):
        other = lax.rem(chip + k, half)
        g = lax.div(other, chips_per_group)
        return rcopy(kvc.at[g], kvin.at[k], kv_s.at[k], kv_r.at[k], other * 2 + core)

    @pl.loop(1, half)
    def _(k):
        kv_copy(k).start()

    @pl.loop(half, n)
    def _(i):
        block = order(i)
        qc(i - half, block, qbuf.at[block]).wait_recv()

    small[2].wait()
    small[3].wait()

    def a1_copy(j):
        return rcopy(att.at[1 - core, j], r1.at[j], a1_s.at[j], a1_r.at[j], sibling)

    def a1s_copy(j):
        return rcopy(
            ast.at[1 - core, j], r1s.at[j], a1_s.at[half + j], a1_r.at[half + j], sibling)

    @pl.loop(0, KVH)
    def _(g):
        lane = pl.ds(pl.multiple_of(g * HD, HD), HD)
        k_g = ck_v[:, :, lane].reshape(keys, HD)
        v_g = cv_v[:, :, lane].reshape(keys, HD)
        q_g = jnp.concatenate([
            qbuf[g * per_group + i // heads_dev, :,
                 (i % heads_dev) * HD:(i % heads_dev + 1) * HD]
            for i in range(GROUP)], axis=0)
        s = dot(k_g, q_g, ((1,), (1,))) * scale + bias[...]
        top = jnp.max(s, axis=0, keepdims=True)
        p = jnp.exp(s - top)
        total = jnp.sum(p, axis=0, keepdims=True)
        a = dot(v_g, p.astype(bf16), ((0,), (0,))).astype(bf16)
        for t in range(per_group):
            j = g * (per_group // 2) + t // 2
            att[t % 2, j] = a[:, t * head_cols:(t + 1) * head_cols]
            ast[t % 2, j, 0:1] = top[:, t * head_cols:(t + 1) * head_cols]
            ast[t % 2, j, 1:2] = total[:, t * head_cols:(t + 1) * head_cols]
        for t in range(per_group // 2):
            a1_copy(g * (per_group // 2) + t).start()
            a1s_copy(g * (per_group // 2) + t).start()

    def triple(values, stats):
        return stats[0:1], stats[1:2], values.astype(f32)

    def chip_part(j):
        a1_copy(j).wait_recv()
        a1s_copy(j).wait_recv()
        return merge(triple(att[core, j], ast[core, j]), triple(r1[j], r1s[j]))

    def a2_copy(z):
        return rcopy(ysend.at[z], r2.at[z], a2_s.at[z], a2_r.at[z], across)

    def a2s_copy(z):
        return rcopy(ysends.at[z], r2s.at[z], a2_s.at[nz + z], a2_r.at[nz + z], across)

    def a3_copy(k):
        return rcopy(zsend.at[k], r3.at[k], a3_s.at[k], a3_r.at[k], rank_of(zmod(k), yy, core))

    def a3s_copy(k):
        return rcopy(
            zsends.at[k], r3s.at[k], a3_s.at[nz + k], a3_r.at[nz + k],
            rank_of(zmod(k), yy, core))

    @pl.loop(0, nz)
    def _(k):
        z = zmod(k + 1)
        m, l, a = chip_part(z * 2 + 1 - yy)
        ysend[z] = a.astype(bf16)
        ysends[z, 0:1] = m
        ysends[z, 1:2] = l
        a2_copy(z).start()
        a2s_copy(z).start()

    def pair_part(z):
        mine = chip_part(z * 2 + yy)
        a2_copy(z).wait_recv()
        a2s_copy(z).wait_recv()
        return merge(mine, triple(r2[z], r2s[z]))

    @pl.loop(1, nz)
    def _(k):
        m, l, a = pair_part(zmod(k))
        zsend[k] = a.astype(bf16)
        zsends[k, 0:1] = m
        zsends[k, 1:2] = l
        a3_copy(k).start()
        a3s_copy(k).start()

    own = pair_part(zz)

    my_group = lax.div(chip, chips_per_group)
    fresh = kvc[my_group].astype(f32)
    for k in range(1, half):
        kv_copy(k).wait_recv()
        fresh = fresh + kvin[k].astype(f32)
    kvf[core] = fresh
    kv_out = rcopy(kvf.at[core], kvf.at[core], kc_s.at[0], kc_r.at[0], sibling)
    kv_out.start()
    rcopy(kvf.at[1 - core], kvf.at[1 - core], kc_s.at[0], kc_r.at[0], sibling).wait_recv()
    fresh_key = rotate(kvf[0] * inverse).astype(bf16)
    fresh_value = (kvf[1] * inverse).astype(bf16)
    q_own = jnp.concatenate(
        [qbuf[me, :, h * HD:(h + 1) * HD] for h in range(heads_dev)], axis=0)
    sf = dot(fresh_key, q_own, ((1,), (1,))) * scale
    frow = lax.broadcasted_iota(jnp.int32, (rows, head_cols), 0)
    fcol = lax.broadcasted_iota(jnp.int32, (rows, head_cols), 1)
    sf = jnp.where(frow == (fcol & (rows - 1)), sf, masked_value)
    top_f = jnp.max(sf, axis=0, keepdims=True)
    pf = jnp.exp(sf - top_f)
    own = merge(own, (
        top_f, jnp.sum(pf, axis=0, keepdims=True),
        dot(fresh_value, pf.astype(bf16), ((0,), (0,)))))
    for k in range(1, nz):
        a3_copy(k).wait_recv()
        a3s_copy(k).wait_recv()
        own = merge(own, triple(r3[k], r3s[k]))
    head_t = jnp.transpose(own[2] / own[1])
    head_rows = jnp.concatenate(
        [head_t[h * rows:(h + 1) * rows] for h in range(heads_dev)], axis=1).astype(bf16)

    @pl.loop(0, n)
    def _(r):
        wo_copy(r).wait()

    def project(r):
        return dot(head_rows, wo_v[r], ((1,), (0,)))

    def o1_copy(i):
        return rcopy(osend.at[i], ro1.at[i], o1_s.at[i], o1_r.at[i], sibling)

    def o2_copy(k):
        return rcopy(oy.at[k], ro2.at[k], o2_s.at[k], o2_r.at[k], across)

    def o3_copy(k):
        return rcopy(oz.at[k], ro3.at[k], o3_s.at[k], o3_r.at[k], rank_of(zmod(k), yy, core))

    def target(i, y_first):
        k = lax.rem(i + 1, nz)
        y = jnp.where(i < nz, y_first, 1 - y_first)
        return zmod(k), y

    @pl.loop(0, half)
    def _(i):
        z, y = target(i, 1 - yy)
        osend[i] = project(rank_of(z, y, 1 - core)).astype(bf16)
        o1_copy(i).start()

    @pl.loop(0, nz)
    def _(i):
        z, y = target(i, 1 - yy)
        value = project(rank_of(z, y, core))
        o1_copy(i).wait_recv()
        oy[i] = (value + ro1[i].astype(f32)).astype(bf16)
        o2_copy(i).start()

    def out_part(i):
        z, y = target(nz + i, 1 - yy)
        value = project(rank_of(z, y, core))
        o1_copy(nz + i).wait_recv()
        value = value + ro1[nz + i].astype(f32)
        o2_copy(i).wait_recv()
        return value + ro2[i].astype(f32)

    @pl.loop(0, nz - 1)
    def _(i):
        oz[i + 1] = out_part(i).astype(bf16)
        o3_copy(i + 1).start()

    summed = out_part(nz - 1)
    for k in range(1, nz):
        o3_copy(k).wait_recv()
        summed = summed + ro3[k].astype(f32)
    hidden = (tok[...].astype(f32) + summed).astype(bf16)
    hidden_out[...] = hidden
    wide = hidden.astype(f32)
    square = jnp.sum(wide * wide, axis=1, keepdims=True)
    diagonal = (
        lax.broadcasted_iota(jnp.int32, (rows, HD), 0)
        == lax.broadcasted_iota(jnp.int32, (rows, HD), 1))
    ss[0] = jnp.sum(jnp.where(diagonal, square, 0.0), axis=0, keepdims=True)

    def ss_copy(k):
        return rcopy(ss.at[0], ss.at[k], ss_s.at[k], ss_r.at[k], lax.rem(me + k, n))

    @pl.loop(1, n)
    def _(k):
        ss_copy(k).start()

    total = ss[0]
    for k in range(1, n):
        ss_copy(k).wait_recv()
        total = total + ss[k]
    mean = jnp.sum(jnp.where(diagonal, total, 0.0), axis=1, keepdims=True) / (n * width)
    normed_out[...] = (wide * lax.rsqrt(mean + epsilon) * pgain[...]).astype(bf16)

    @pl.loop(1, nz)
    def _(k):
        tz(k).wait_send()
        qz(k).wait_send()
        a3_copy(k).wait_send()
        a3s_copy(k).wait_send()
        o3_copy(k).wait_send()

    @pl.loop(0, nz)
    def _(k):
        ty(k, tok).wait_send()
        qy(k, own_q).wait_send()
        a2_copy(k).wait_send()
        a2s_copy(k).wait_send()
        o2_copy(k).wait_send()

    @pl.loop(0, half)
    def _(k):
        tc(k, me, tok).wait_send()
        qc(k, me, own_q).wait_send()
        a1_copy(k).wait_send()
        a1s_copy(k).wait_send()
        o1_copy(k).wait_send()

    @pl.loop(1, half)
    def _(k):
        kv_copy(k).wait_send()

    @pl.loop(1, n)
    def _(k):
        ss_copy(k).wait_send()

    kv_pair.wait_send()
    kv_out.wait_send()


def local(n, tokens, in_gain, w_query, w_key, w_value, w_out, cache_keys, cache_values, lengths,
          post_gain):
    rows, width = tokens.shape
    cols = w_query.shape[1]
    span = cache_keys.shape[1]
    kv_width = w_key.shape[1]
    heads_dev = cols // HD
    head_cols = heads_dev * rows
    nz, half = n // 4, n // 2
    exponents = jnp.arange(HD // 2, dtype=f32) * (2.0 / HD)
    frequency = jnp.power(f32(rotary_base), -exponents)
    angles = lengths.astype(f32)[:, None] * frequency[None, :]
    cosine, sine = jnp.cos(angles), jnp.sin(angles)
    cosine = jnp.concatenate([cosine, cosine], axis=1)
    sine = jnp.concatenate([-sine, sine], axis=1)
    lens = jnp.tile(lengths, GROUP)[None, :]
    vm = pl.BlockSpec(memory_space=pltpu.VMEM)
    hbm = pl.BlockSpec(memory_space=pl.ANY)
    V = pltpu.VMEM
    dma = lambda k: pltpu.SemaphoreType.DMA((k,))
    attn = lambda k: V((k, HD, head_cols), bf16)
    stat = lambda k: V((k, 2, head_cols), f32)
    block = lambda k: V((k, rows, width), bf16)
    scratch = [
        V((n, width, cols), bf16), V((width, kv_width), bf16), V((width, kv_width), bf16),
        V((n, cols, width), bf16), V(cache_keys.shape, bf16), V(cache_values.shape, bf16),
        block(n), V((n, rows, cols), bf16), V((rows, cols), f32), V((rows, HD), f32),
        V((rows * span, GROUP * rows), f32),
        V((2, KVH, rows, HD), bf16), V((KVH, rows, HD), bf16), V((KVH, rows, HD), bf16),
        V((half, rows, HD), bf16), V((2, rows, HD), f32),
        V((2, half, HD, head_cols), bf16), V((2, half, 2, head_cols), f32),
        attn(half), stat(half), attn(nz), stat(nz), attn(nz), stat(nz), attn(nz), stat(nz),
        attn(nz), stat(nz),
        block(half), block(half), block(nz), block(nz), block(nz), block(nz),
        V((n, 1, HD), f32),
        dma(4), dma(n), dma(n),
        dma(nz), dma(nz), dma(nz), dma(nz), dma(half), dma(half),
        dma(nz), dma(nz), dma(nz), dma(nz), dma(half), dma(half),
        dma(half), dma(half), dma(1), dma(1),
        dma(n), dma(n), dma(half), dma(half), dma(half), dma(half),
        dma(half), dma(half), dma(nz), dma(nz), dma(nz), dma(nz), dma(n), dma(n),
    ]
    return pl.pallas_call(
        functools.partial(kernel, n, rows, width, cols, span),
        out_shape=(jax.ShapeDtypeStruct((rows, width), bf16),) * 2,
        in_specs=[vm, vm, hbm, hbm, hbm, hbm, hbm, hbm, vm, vm, vm, vm],
        out_specs=(vm, vm),
        scratch_shapes=scratch,
        compiler_params=pltpu.CompilerParams(
            collective_id=0, has_side_effects=True, vmem_limit_bytes=67043328),
    )(
        tokens, in_gain.astype(f32)[None, :], w_query, w_key, w_value, w_out, cache_keys,
        cache_values, lens, cosine, sine, post_gain.astype(f32)[None, :],
    )


def solution(mesh):
    placed = (
        P("replica", "tp"),
        P(),
        P(None, "tp"),
        P("tp", None),
        P("tp", None),
        P("tp", None),
        P("replica", "tp", None),
        P("replica", "tp", None),
        P("replica"),
        P("tp"),
    )
    return jax.shard_map(
        functools.partial(local, mesh.shape["tp"]),
        mesh=mesh,
        in_specs=placed,
        out_specs=(P("replica", "tp"), P("replica", "tp")),
        check_vma=False,
    )
```

time: 333 us -> 71.6 us (0.22)
  blocking collectives: 139 us -> 0 us
  waiting for transfers between devices: 136 us -> 0 us
  Pallas kernels: 0 us -> 62.2 us
  matrix products: 24.2 us -> 0 us
  between operations: 14.6 us -> 0.64 us
  other arithmetic: 11.6 us -> 4.17 us
    psum x2 -> x0, waiting for transfers between devices: 94.9 us -> none  [the longest x1 94.9 us: local(): summed = lax.psum(projected, 'tp')]
    pallas_call x0 -> x1, Pallas kernels: none -> 62.2 us  [local(): pl.pallas_call(functools.partial(kernel, n, rows, width, cols, span), out...]
    unnamed x1 -> x0, blocking collectives: 59.6 us -> none
    pmax x1 -> x0, blocking collectives: 58.8 us -> none  [local(): cache_peak = lax.pmax(jnp.max(masked, axis=-1), 'tp')]
    all_gather x1 -> x0, waiting for transfers between devices: 40.5 us -> none  [local(): gathered = lax.all_gather(tokens, 'tp', axis=1, tiled=True)]
    dot_general x7 -> x0, matrix products: 24.2 us -> none  [the longest x1 10.2 us: local(): projected = jnp.dot(head_rows, w_out, preferred_element_type=jnp.float32)]
    all_gather x1 -> x0, blocking collectives: 21 us -> none  [local(): lax.all_gather(own_query.reshape(batch_rows, heads_dev * HD), 'tp', axis=...]
    reduce_sum x3 -> x0, other arithmetic: 4.19 us -> none  [the longest x2 3.54 us: inverse_rms(): jnp.mean(rows_wide * rows_wide, axis=-1, keepdims=True) + epsilon]
  transfers between devices with their start and end apart: 4 -> 0, of which waited for: 2 -> 0; matrix products, arithmetic and copies ran while one was open for 5% -> 0% of each run, Pallas kernels for 0% -> 0%
where the time goes in v1:
time: 71.6 us; the launch traced here: 71.2 us
  Pallas kernels  62.2 us (87%)
  local copies, waits for them, and re-layouts  4.21 us (6%)
  other arithmetic  4.17 us (6%)
    pallas_call x1, Pallas kernels, local(): pl.pallas_call(functools.partial(kernel, n, rows, width, cols, span), out...  62.2 us
    unnamed x2, local copies, waits for them, and re-layouts  2.95 us

profile of v1, /device:TPU:0, one launch (start us, length us, event | category | flops | bytes accessed | tf_op | source)
XLA Modules:
  0.0 71.2 jit_solution(4153436219267328950)
XLA Ops:
  0.6 0.7 convert_element_type.2
  1.3 1.3 %broadcast_in_dim.17 = f32[1024]{0:T(1024)} convert(bf16[1024]{0:T(1024)(128)(2,1)} %param.19) | non-fusion elementwise | flops 1024 | bytes 6144 | tf_op jit(solution)/shard_map/broadcast_in_dim | solution.py:521
  2.6 0.7 tile.2
  3.2 0.6 broadcast_in_dim_tile.3.lens
  3.8 0.1 fusion
  4.0 0.7 pad_maximum_fusion
  4.7 1.4 %broadcast_in_dim.16 = f32[16384]{0:T(1024)} convert(bf16[16384]{0:T(1024)(128)(2,1)} %param.11) | non-fusion elementwise | flops 16384 | bytes 98304 | tf_op jit(solution)/shard_map/broadcast_in_dim | solution.py:520
  6.1 62.2 %shard_map.113 = (bf16[32,1024]{1,0:T(8,128)(2,1)}, bf16[32,1024]{1,0:T(8,128)(2,1)}) custom-call(bf16[32,1024]{1,0:T(8,128)(2,1)} %tok.1, f32[1,16384]{1,0:T(1,128)} %bitcast.2, bf16[16384,512]{1,0:T(8,128)(2,1)} %wq.1, bf16[1024,1024]{1,0:T(8,128)(2,1)} %wk.1, bf16[1024,1024]{1,0:T(8,128)(2,1)} %wv.1, bf16[512,16384]{1,0:T(8,128)(2,1)} %wo.1, ...), custom_call_target="tpu_custom_call" | custom-call | tf_op jit(solution)/shard_map/pallas_call | solution.py:511
  68.3 1.5 %copy.14 = bf16[32,1024]{1,0:T(8,128)(2,1)} copy(bf16[32,1024]{1,0:T(8,128)(2,1)} %get-tuple-element.9) | data formatting | bytes 131072
  69.8 1.5 %copy.15 = bf16[32,1024]{1,0:T(8,128)(2,1)} copy(bf16[32,1024]{1,0:T(8,128)(2,1)} %get-tuple-element.10) | data formatting | bytes 131072
  (1 shorter events, 0.0 us)

commit v2 on v1

--- a/solution.py
+++ b/solution.py
@@ -40,8 +40,9 @@
 
 def kernel(
     n, rows, width, cols, span,
-    tok, gain, wq, wk, wv, wo, ck, cv, lens, cosine, sine, pgain,
-    hidden_out, normed_out,
+    tok, gain_in, post_in, lens_in, wq, wk, wv, wo, ck, cv,
+    out,
+    gain, cosine, sine, hid_v, nrm_v, s_out,
     wq_v, wk_v, wv_v, wo_v, ck_v, cv_v, tokbuf, qbuf, acc, ssq, bias,
     kvp, kvr, kvc, kvin, kvf,
     att, ast, r1, r1s, ysend, ysends, r2, r2s, zsend, zsends, r3, r3s,
@@ -71,6 +72,9 @@
     def zmod(k):
         return lax.rem(zz + k, nz)
 
+    def off(i):
+        return lax.rem(jnp.where(zz >= nz // 2, i, nz - i), nz)
+
     sibling = rank_of(zz, yy, 1 - core)
     across = rank_of(zz, 1 - yy, core)
 
@@ -79,7 +83,7 @@
         part = lax.div(index, nz)
         y = jnp.where(lax.rem(part, 2) == 0, yy, 1 - yy)
         c = jnp.where(part < 2, core, 1 - core)
-        return rank_of(zmod(nz - k), y, c)
+        return rank_of(zmod(nz - off(k)), y, c)
 
     def wq_copy(index):
         block = order(index)
@@ -95,15 +99,13 @@
         pltpu.make_async_copy(a, b, s_w.at[i])
         for i, (a, b) in enumerate(((wk, wk_v), (wv, wv_v), (ck, ck_v), (cv, cv_v)))
     ]
-    small[0].start()
-    small[1].start()
-
-    @pl.loop(0, n)
+    @pl.loop(0, half)
     def _(index):
         wq_copy(index).start()
-
-    small[2].start()
-    small[3].start()
+        wq_copy(half + index).start()
+
+    for copy in small:
+        copy.start()
 
     barrier = pltpu.get_barrier_semaphore()
 
@@ -113,6 +115,25 @@
             barrier, inc=1, device_id={"tp": lax.rem(me + k, n)},
             device_id_type=pl.DeviceIdType.MESH)
 
+    wide_gain = gain_in[...].astype(f32)
+    for i in range(n * width // HD):
+        gain[:, i * HD:(i + 1) * HD] = wide_gain[i:i + 1]
+    sub = lax.broadcasted_iota(jnp.int32, (rows, rows), 0)
+    lane_b = lax.broadcasted_iota(jnp.int32, (rows, rows), 1)
+    len_column = jnp.sum(
+        jnp.where(sub == lane_b, lens_in[...].astype(f32), 0.0), axis=1, keepdims=True)
+    lanes = GROUP * rows
+    sub = lax.broadcasted_iota(jnp.int32, (rows, lanes), 0)
+    lane_b = lax.broadcasted_iota(jnp.int32, (rows, lanes), 1) & (rows - 1)
+    lens = jnp.sum(jnp.where(sub == lane_b, len_column, 0.0), axis=0, keepdims=True)
+    lane = lax.broadcasted_iota(jnp.int32, (rows, HD), 1)
+    exponent = (lane & (HD // 2 - 1)).astype(f32) * (2.0 / HD)
+    angle = len_column * jnp.exp(exponent * (-math.log(rotary_base)))
+    cosine[...] = jnp.cos(angle)
+    sine[...] = jnp.where(lane < HD // 2, -1.0, 1.0) * jnp.sin(angle)
+    acc[...] = jnp.zeros_like(acc)
+    ssq[...] = jnp.zeros_like(ssq)
+
     pl.semaphore_wait(barrier, n - 1)
 
     def gather_copies(own, buf, zs, zr, ys, yr, cs, cr):
@@ -120,7 +141,7 @@
             return rcopy(own, buf.at[me], zs.at[k], zr.at[k], rank_of(zmod(k), yy, core))
 
         def y_copy(k, src):
-            block = rank_of(zmod(nz - k), yy, core)
+            block = rank_of(zmod(nz - off(k)), yy, core)
             return rcopy(src, buf.at[block], ys.at[k], yr.at[k], across)
 
         def c_copy(i, block, src):
@@ -132,7 +153,7 @@
 
     @pl.loop(1, nz)
     def _(k):
-        tz(k).start()
+        tz(off(k)).start()
 
     ty(0, tok).start()
     tc(0, me, tok).start()
@@ -145,8 +166,54 @@
         wq_copy(index).wait()
         acc[...] += dot(scaled, wq_v[index], ((1,), (0,)))
 
-    acc[...] = jnp.zeros_like(acc)
-    ssq[...] = jnp.zeros_like(ssq)
+    use_block(0, tok[...])
+
+    def use_sibling(i):
+        block = order(half + i)
+        tc(i, block, tokbuf.at[block]).wait_recv()
+        use_block(half + i, tokbuf[block])
+
+    @pl.loop(1, nz)
+    def _(k):
+        tz(off(k)).wait_recv()
+        block = order(k)
+        ty(k, tokbuf.at[block]).start()
+        tc(k, block, tokbuf.at[block]).start()
+        use_block(k, tokbuf[block])
+        use_sibling(k - 1)
+
+    @pl.loop(0, nz)
+    def _(k):
+        block = order(nz + k)
+        ty(k, tokbuf.at[block]).wait_recv()
+        tc(nz + k, block, tokbuf.at[block]).start()
+        use_block(nz + k, tokbuf[block])
+        use_sibling(nz + k - 1)
+
+    @pl.loop(0, n)
+    def _(r):
+        wo_copy(r).start()
+
+    use_sibling(half - 1)
+
+    inverse = lax.rsqrt(jnp.sum(ssq[...], axis=1, keepdims=True) / (n * width) + epsilon)
+
+    def rotate(v):
+        return v * cosine[...] + pltpu.roll(v, HD // 2, 1) * sine[...]
+
+    for h in range(heads_dev):
+        qbuf[me, :, h * HD:(h + 1) * HD] = rotate(
+            acc[:, h * HD:(h + 1) * HD] * inverse).astype(bf16)
+
+    own_q = qbuf.at[me]
+    qz, qy, qc = gather_copies(own_q, qbuf, qz_s, qz_r, qy_s, qy_r, qc_s, qc_r)
+
+    @pl.loop(1, nz)
+    def _(k):
+        qz(off(k)).start()
+
+    qy(0, own_q).start()
+    qc(0, me, own_q).start()
 
     own_in = (
         tok[...].astype(f32) * gain[:, pl.ds(pl.multiple_of(me * width, width), width)]
@@ -158,64 +225,18 @@
             kvp[i, g] = part[:, g * HD:(g + 1) * HD]
     kv_pair = rcopy(kvp.at[1 - core], kvr, kv_s.at[0], kv_r.at[0], sibling)
     kv_pair.start()
-    use_block(0, tok[...])
-
-    @pl.loop(1, nz)
-    def _(k):
-        tz(k).wait_recv()
-        block = order(k)
-        ty(k, tokbuf.at[block]).start()
-        tc(k, block, tokbuf.at[block]).start()
-        use_block(k, tokbuf[block])
-
-    @pl.loop(0, nz)
-    def _(k):
-        block = order(nz + k)
-        ty(k, tokbuf.at[block]).wait_recv()
-        tc(nz + k, block, tokbuf.at[block]).start()
-        use_block(nz + k, tokbuf[block])
-
-    @pl.loop(0, n)
-    def _(r):
-        wo_copy(r).start()
-
-    @pl.loop(half, n)
-    def _(i):
-        block = order(i)
-        tc(i - half, block, tokbuf.at[block]).wait_recv()
-        use_block(i, tokbuf[block])
-
-    inverse = lax.rsqrt(jnp.sum(ssq[...], axis=1, keepdims=True) / (n * width) + epsilon)
-
-    def rotate(v):
-        return v * cosine[...] + pltpu.roll(v, HD // 2, 1) * sine[...]
-
-    for h in range(heads_dev):
-        qbuf[me, :, h * HD:(h + 1) * HD] = rotate(
-            acc[:, h * HD:(h + 1) * HD] * inverse).astype(bf16)
-
-    own_q = qbuf.at[me]
-    qz, qy, qc = gather_copies(own_q, qbuf, qz_s, qz_r, qy_s, qy_r, qc_s, qc_r)
-
-    @pl.loop(1, nz)
-    def _(k):
-        qz(k).start()
-
-    qy(0, own_q).start()
-    qc(0, me, own_q).start()
 
     keys = rows * span
-    lanes = GROUP * rows
     row = lax.broadcasted_iota(jnp.int32, (keys, lanes), 0)
     column = lax.broadcasted_iota(jnp.int32, (keys, lanes), 1)
     shift = span.bit_length() - 1
     same = lax.shift_right_logical(row, shift) == (column & (rows - 1))
-    seen = (me * span + (row & (span - 1))) < lens[...]
+    seen = (me * span + (row & (span - 1))).astype(f32) < lens
     bias[...] = jnp.where(same & seen, 0.0, masked_value)
 
     @pl.loop(1, nz)
     def _(k):
-        qz(k).wait_recv()
+        qz(off(k)).wait_recv()
         block = order(k)
         qy(k, qbuf.at[block]).start()
         qc(k, block, qbuf.at[block]).start()
@@ -253,8 +274,7 @@
         return rcopy(
             ast.at[1 - core, j], r1s.at[j], a1_s.at[half + j], a1_r.at[half + j], sibling)
 
-    @pl.loop(0, KVH)
-    def _(g):
+    def attend(g):
         lane = pl.ds(pl.multiple_of(g * HD, HD), HD)
         k_g = ck_v[:, :, lane].reshape(keys, HD)
         v_g = cv_v[:, :, lane].reshape(keys, HD)
@@ -298,9 +318,19 @@
             zsends.at[k], r3s.at[k], a3_s.at[nz + k], a3_r.at[nz + k],
             rank_of(zmod(k), yy, core))
 
-    @pl.loop(0, nz)
-    def _(k):
-        z = zmod(k + 1)
+    kv_out = rcopy(kvf.at[core], kvf.at[core], kc_s.at[0], kc_r.at[0], sibling)
+
+    def sum_fresh():
+        my_group = lax.div(chip, chips_per_group)
+        fresh = kvc[my_group].astype(f32)
+        for k in range(1, half):
+            kv_copy(k).wait_recv()
+            fresh = fresh + kvin[k].astype(f32)
+        kvf[core] = fresh
+        kv_out.start()
+
+    def y_stage(k):
+        z = zmod(off(lax.rem(k + 1, nz)))
         m, l, a = chip_part(z * 2 + 1 - yy)
         ysend[z] = a.astype(bf16)
         ysends[z, 0:1] = m
@@ -314,8 +344,8 @@
         a2s_copy(z).wait_recv()
         return merge(mine, triple(r2[z], r2s[z]))
 
-    @pl.loop(1, nz)
-    def _(k):
+    def z_stage(i):
+        k = off(i)
         m, l, a = pair_part(zmod(k))
         zsend[k] = a.astype(bf16)
         zsends[k, 0:1] = m
@@ -323,16 +353,35 @@
         a3_copy(k).start()
         a3s_copy(k).start()
 
+    if half == KVH:
+        def send_order(i):
+            y = jnp.where(i < nz, 1 - yy, yy)
+            return zmod(off(lax.rem(i + 1, nz))) * 2 + y
+
+        attend(send_order(0))
+        attend(send_order(1))
+
+        @pl.loop(0, nz)
+        def _(k):
+            attend(send_order(k + 2))
+            y_stage(k)
+
+        sum_fresh()
+
+        @pl.loop(1, nz - 1)
+        def _(k):
+            attend(send_order(nz + k + 1))
+            z_stage(k)
+
+        z_stage(nz - 1)
+    else:
+        pl.loop(0, KVH)(attend)
+        pl.loop(0, nz)(y_stage)
+        sum_fresh()
+        pl.loop(1, nz)(z_stage)
+
     own = pair_part(zz)
 
-    my_group = lax.div(chip, chips_per_group)
-    fresh = kvc[my_group].astype(f32)
-    for k in range(1, half):
-        kv_copy(k).wait_recv()
-        fresh = fresh + kvin[k].astype(f32)
-    kvf[core] = fresh
-    kv_out = rcopy(kvf.at[core], kvf.at[core], kc_s.at[0], kc_r.at[0], sibling)
-    kv_out.start()
     rcopy(kvf.at[1 - core], kvf.at[1 - core], kc_s.at[0], kc_r.at[0], sibling).wait_recv()
     fresh_key = rotate(kvf[0] * inverse).astype(bf16)
     fresh_value = (kvf[1] * inverse).astype(bf16)
@@ -372,18 +421,20 @@
         return rcopy(oz.at[k], ro3.at[k], o3_s.at[k], o3_r.at[k], rank_of(zmod(k), yy, core))
 
     def target(i, y_first):
-        k = lax.rem(i + 1, nz)
+        k = off(lax.rem(i + 1, nz))
         y = jnp.where(i < nz, y_first, 1 - y_first)
         return zmod(k), y
 
-    @pl.loop(0, half)
-    def _(i):
+    def for_sibling(i):
         z, y = target(i, 1 - yy)
         osend[i] = project(rank_of(z, y, 1 - core)).astype(bf16)
         o1_copy(i).start()
 
+    for_sibling(0)
+
     @pl.loop(0, nz)
     def _(i):
+        for_sibling(i + 1)
         z, y = target(i, 1 - yy)
         value = project(rank_of(z, y, core))
         o1_copy(i).wait_recv()
@@ -400,16 +451,20 @@
 
     @pl.loop(0, nz - 1)
     def _(i):
-        oz[i + 1] = out_part(i).astype(bf16)
-        o3_copy(i + 1).start()
+        for_sibling(nz + i + 1)
+        k = off(i + 1)
+        oz[k] = out_part(i).astype(bf16)
+        o3_copy(k).start()
 
     summed = out_part(nz - 1)
     for k in range(1, nz):
         o3_copy(k).wait_recv()
         summed = summed + ro3[k].astype(f32)
     hidden = (tok[...].astype(f32) + summed).astype(bf16)
-    hidden_out[...] = hidden
     wide = hidden.astype(f32)
+    hid_v[...] = hidden
+    hid_copy = pltpu.make_async_copy(hid_v, out.at[0], s_out.at[0])
+    hid_copy.start()
     square = jnp.sum(wide * wide, axis=1, keepdims=True)
     diagonal = (
         lax.broadcasted_iota(jnp.int32, (rows, HD), 0)
@@ -428,7 +483,13 @@
         ss_copy(k).wait_recv()
         total = total + ss[k]
     mean = jnp.sum(jnp.where(diagonal, total, 0.0), axis=1, keepdims=True) / (n * width)
-    normed_out[...] = (wide * lax.rsqrt(mean + epsilon) * pgain[...]).astype(bf16)
+    row_scale = lax.rsqrt(mean + epsilon)
+    post = post_in[...].astype(f32)
+    for i in range(width // HD):
+        part = slice(i * HD, (i + 1) * HD)
+        nrm_v[:, part] = (wide[:, part] * row_scale * post[i:i + 1]).astype(bf16)
+    nrm_copy = pltpu.make_async_copy(nrm_v, out.at[1], s_out.at[1])
+    nrm_copy.start()
 
     @pl.loop(1, nz)
     def _(k):
@@ -464,6 +525,8 @@
 
     kv_pair.wait_send()
     kv_out.wait_send()
+    hid_copy.wait()
+    nrm_copy.wait()
 
 
 def local(n, tokens, in_gain, w_query, w_key, w_value, w_out, cache_keys, cache_values, lengths,
@@ -475,13 +538,6 @@
     heads_dev = cols // HD
     head_cols = heads_dev * rows
     nz, half = n // 4, n // 2
-    exponents = jnp.arange(HD // 2, dtype=f32) * (2.0 / HD)
-    frequency = jnp.power(f32(rotary_base), -exponents)
-    angles = lengths.astype(f32)[:, None] * frequency[None, :]
-    cosine, sine = jnp.cos(angles), jnp.sin(angles)
-    cosine = jnp.concatenate([cosine, cosine], axis=1)
-    sine = jnp.concatenate([-sine, sine], axis=1)
-    lens = jnp.tile(lengths, GROUP)[None, :]
     vm = pl.BlockSpec(memory_space=pltpu.VMEM)
     hbm = pl.BlockSpec(memory_space=pl.ANY)
     V = pltpu.VMEM
@@ -490,6 +546,8 @@
     stat = lambda k: V((k, 2, head_cols), f32)
     block = lambda k: V((k, rows, width), bf16)
     scratch = [
+        V((1, n * width), f32), V((rows, HD), f32), V((rows, HD), f32),
+        V((rows, width), bf16), V((rows, width), bf16), dma(2),
         V((n, width, cols), bf16), V((width, kv_width), bf16), V((width, kv_width), bf16),
         V((n, cols, width), bf16), V(cache_keys.shape, bf16), V(cache_values.shape, bf16),
         block(n), V((n, rows, cols), bf16), V((rows, cols), f32), V((rows, HD), f32),
@@ -508,18 +566,19 @@
         dma(n), dma(n), dma(half), dma(half), dma(half), dma(half),
         dma(half), dma(half), dma(nz), dma(nz), dma(nz), dma(nz), dma(n), dma(n),
     ]
-    return pl.pallas_call(
+    both = pl.pallas_call(
         functools.partial(kernel, n, rows, width, cols, span),
-        out_shape=(jax.ShapeDtypeStruct((rows, width), bf16),) * 2,
-        in_specs=[vm, vm, hbm, hbm, hbm, hbm, hbm, hbm, vm, vm, vm, vm],
-        out_specs=(vm, vm),
+        out_shape=jax.ShapeDtypeStruct((2, rows, width), bf16),
+        in_specs=[vm, vm, vm, vm, hbm, hbm, hbm, hbm, hbm, hbm],
+        out_specs=hbm,
         scratch_shapes=scratch,
         compiler_params=pltpu.CompilerParams(
             collective_id=0, has_side_effects=True, vmem_limit_bytes=67043328),
     )(
-        tokens, in_gain.astype(f32)[None, :], w_query, w_key, w_value, w_out, cache_keys,
-        cache_values, lens, cosine, sine, post_gain.astype(f32)[None, :],
+        tokens, in_gain.reshape(-1, HD), post_gain.reshape(-1, HD), lengths[None, :], w_query,
+        w_key, w_value, w_out, cache_keys, cache_values,
     )
+    return both[0], both[1]
 
 
 def solution(mesh):

time: 71.6 us -> 61.7 us (0.86)
  other arithmetic: 4.17 us -> 0 us
  Pallas kernels: 62.2 us -> 59.3 us
  local copies, waits for them, and re-layouts: 4.21 us -> 1.53 us
    unnamed x2 -> x0, local copies, waits for them, and re-layouts: 2.95 us -> none
    pallas_call x1, Pallas kernels: 62.2 us -> 59.3 us  [local(): pl.pallas_call(functools.partial(kernel, n, rows, width, cols, span), out...]
    broadcast_in_dim x2 -> x0, other arithmetic: 2.66 us -> none  [the longest x1 1.39 us: local(): in_gain.astype(f32)[None, :]]
    squeeze x0 -> x1, local copies, waits for them, and re-layouts: none -> 1.53 us  [local(): return (both[0], both[1])]
    another operation x2 -> x0, local copies, waits for them, and re-layouts: 1.27 us -> none  [local(): lens = jnp.tile(lengths, GROUP)[None, :]]
where the time goes in v2:
time: 61.7 us; the launch traced here: 61.5 us
  Pallas kernels  59.3 us (96%)
  local copies, waits for them, and re-layouts  1.53 us (2%)
  between operations  0.64 us (1%)
    pallas_call x1, Pallas kernels, local(): pl.pallas_call(functools.partial(kernel, n, rows, width, cols, span), out...  59.3 us
    squeeze x1, local copies, waits for them, and re-layouts, local(): return (both[0], both[1])  1.53 us

profile of v2, /device:TPU:0, one launch (start us, length us, event | category | flops | bytes accessed | tf_op | source)
XLA Modules:
  0.0 61.5 jit_solution(17445667422237639968)
XLA Ops:
  0.6 59.3 %shard_map.113 = bf16[2,32,1024]{2,1,0:T(8,128)(2,1)} custom-call(bf16[32,1024]{1,0:T(8,128)(2,1)} %tok.1, bf16[128,128]{1,0:T(8,128)(2,1)} %bitcast.7, bf16[8,128]{1,0:T(8,128)(2,1)} %bitcast.8, s32[1,32]{1,0:T(1,128)} %bitcast.9, bf16[16384,512]{1,0:T(8,128)(2,1)} %wq.1, bf16[1024,1024]{1,0:T(8,128)(2,1)} %wk.1, bf16[1024,1024]{1,0:T(8,128)(2,1)} %wv.1, ...), custom_call_target="tpu_custom_call" | custom-call | tf_op jit(solution)/shard_map/pallas_call | solution.py:569
  60.0 1.5 %slice_bitcast_fusion = (bf16[32,1024]{1,0:T(8,128)(2,1)}, bf16[32,1024]{1,0:T(8,128)(2,1)}) fusion(bf16[2,32,1024]{2,1,0:T(8,128)(2,1)} %shard_map.113), kind=kLoop, calls=%fused_computation | loop fusion | bytes 262144 | tf_op jit(solution)/shard_map/squeeze | solution.py:581
